TPU v7x, 32 devices: a whole 2x2x4 slice. The times are simulated.
32 devices in a mesh: gx: 4 (over x, core), gy: 4 (over z), gz: 2 (over y).
Axes of the slice: x: 2, y: 2, z: 4, core: 2. Of those that a mesh axis runs over, the one named last changes fastest.
Arguments:
- conserved_state: float32 [6, 16, 32, 240], P(None, 'gx', 'gy', 'gz'), as said below
Outputs:
- updated_state: float32 [6, 16, 32, 240], P(None, 'gx', 'gy', 'gz')
- next_timestep: float32 [], replicated
Inputs may be any that keep to these rules, and one draw needn't show every extreme that they name: `conserved_state`: component 0 is density within 0.5 to 3, components 1 to 3 are density times velocities each within -1 to 1, component 4 is total energy with pressure within 0.5 to 6, component 5 is density times a tracer fraction within 0 to 1.
All inputs are finite; a program needn't handle non-finite values.
Results may differ from a plain program's by a relative error of at most 0.0003.
Values sent between devices are 32-bit elements; how exact they have to be, the bound alone decides.
A program may use at most 64 MiB of HBM per device.

v0:
```python
import jax
import jax.numpy as jnp
from jax import lax
from jax.sharding import PartitionSpec as P

GHOST = 4


adiabatic = 5.0 / 3.0
courant = 0.3


def padded_2(block, sides, width):
    for axis, dim in sides:
        count = lax.axis_size(axis)
        forward = [(i, i + 1) for i in range(count - 1)]
        forward.append((count - 1, 0))
        backward = [(target, source) for source, target in forward]
        low = lax.ppermute(
            lax.slice_in_dim(block, block.shape[dim] - width, None, axis=dim), axis, forward
        )
        high = lax.ppermute(lax.slice_in_dim(block, 0, width, axis=dim), axis, backward)
        block = jnp.concatenate([low, block, high], axis=dim)
    return block


def window(values, axis_number, start, length):
    return lax.slice_in_dim(values, start, start + length, axis=axis_number)


def primitive_of(conserved_list):
    density = conserved_list[0]
    inverse = 1.0 / density
    velocity = [conserved_list[component] * inverse for component in (1, 2, 3)]
    kinetic = 0.5 * (
        conserved_list[1] * velocity[0]
        + conserved_list[2] * velocity[1]
        + conserved_list[3] * velocity[2]
    )
    pressure = (adiabatic - 1.0) * (conserved_list[4] - kinetic)
    return [density, velocity[0], velocity[1], velocity[2], pressure, conserved_list[5] * inverse]


def conserved_of(primitive):
    density = primitive[0]
    momenta = [density * primitive[component] for component in (1, 2, 3)]
    kinetic = 0.5 * (
        momenta[0] * primitive[1] + momenta[1] * primitive[2] + momenta[2] * primitive[3]
    )
    energy = primitive[4] / (adiabatic - 1.0) + kinetic
    return [density, momenta[0], momenta[1], momenta[2], energy, density * primitive[5]]


def fastest_signal(conserved_list):
    primitive = primitive_of(conserved_list)
    sound = jnp.sqrt(adiabatic * primitive[4] / primitive[0])
    speeds = jnp.maximum(
        jnp.maximum(jnp.abs(primitive[1]), jnp.abs(primitive[2])), jnp.abs(primitive[3])
    )
    return jnp.max(speeds + sound)


def parabola(centre, sweep_axis):
    extent = centre.shape[sweep_axis]
    count = extent - 5

    def offset_cells(offset):
        return window(centre, sweep_axis, 3 + offset, count)

    before_one = offset_cells(-1)
    middle = offset_cells(0)
    edge = (
        37.0 * (before_one + middle)
        - 8.0 * (offset_cells(-2) + offset_cells(1))
        + (offset_cells(-3) + offset_cells(2))
    ) / 60.0
    edge = jnp.clip(edge, jnp.minimum(before_one, middle), jnp.maximum(before_one, middle))
    lower = window(edge, sweep_axis, 0, count - 1)
    upper = window(edge, sweep_axis, 1, count - 1)
    inner = window(centre, sweep_axis, 3, count - 1)
    flatten = (upper - inner) * (inner - lower) <= 0.0
    spread = upper - lower
    skewed = spread * (inner - 0.5 * (lower + upper))
    limit = spread * spread / 6.0
    new_lower = jnp.where(
        flatten, inner, jnp.where(skewed > limit, 3.0 * inner - 2.0 * upper, lower)
    )
    new_upper = jnp.where(
        flatten, inner, jnp.where(skewed < -limit, 3.0 * inner - 2.0 * lower, upper)
    )
    return (new_lower, new_upper)


def traced_faces(primitive, sweep_axis, time_step):
    normal = 1 + sweep_axis
    extent = primitive[0].shape[sweep_axis]
    edges = [parabola(item, sweep_axis) for item in primitive]
    slopes = [pair[1] - pair[0] for pair in edges]
    inner = [window(item, sweep_axis, 3, extent - 6) for item in primitive]
    normal_vel = inner[normal]
    density = inner[0]
    rates = [-(normal_vel * slopes[0] + density * slopes[normal])]
    for component in (1, 2, 3):
        if component == normal:
            rates.append(-(normal_vel * slopes[normal] + slopes[4] / density))
        else:
            rates.append(-normal_vel * slopes[component])
    rates.append(-(adiabatic * inner[4] * slopes[normal] + normal_vel * slopes[4]))
    rates.append(-normal_vel * slopes[5])
    lower_faces = [
        edges[component][0] + 0.5 * time_step * rates[component] for component in range(6)
    ]
    upper_faces = [
        edges[component][1] + 0.5 * time_step * rates[component] for component in range(6)
    ]
    return (lower_faces, upper_faces)


def physical_flux(primitive, conserved_list, normal):
    normal_vel = primitive[normal]
    result = [item * normal_vel for item in conserved_list]
    result[normal] = result[normal] + primitive[4]
    result[4] = result[4] + primitive[4] * normal_vel
    return result


def star_state(primitive, conserved_list, outer_speed, middle_speed, normal):
    mass_rate = primitive[0] * (outer_speed - primitive[normal])
    factor = mass_rate / (outer_speed - middle_speed)
    result = [factor * primitive[component] for component in range(6)]
    result[0] = factor
    result[normal] = factor * middle_speed
    result[4] = factor * (
        conserved_list[4] / primitive[0]
        + (middle_speed - primitive[normal]) * (middle_speed + primitive[4] / mass_rate)
    )
    return result


def hllc_flux(left, right, sweep_axis):
    normal = 1 + sweep_axis
    sound_left = jnp.sqrt(adiabatic * left[4] / left[0])
    sound_right = jnp.sqrt(adiabatic * right[4] / right[0])
    low_speed = jnp.minimum(left[normal] - sound_left, right[normal] - sound_right)
    high_speed = jnp.maximum(left[normal] + sound_left, right[normal] + sound_right)
    mass_left = left[0] * (low_speed - left[normal])
    mass_right = right[0] * (high_speed - right[normal])
    middle = (right[4] - left[4] + mass_left * left[normal] - mass_right * right[normal]) / (
        mass_left - mass_right
    )
    left_state = conserved_of(left)
    right_state = conserved_of(right)
    flux_left = physical_flux(left, left_state, normal)
    flux_right = physical_flux(right, right_state, normal)
    star_left = star_state(left, left_state, low_speed, middle, normal)
    star_right = star_state(right, right_state, high_speed, middle, normal)
    result = []
    for component in range(6):
        left_star_flux = flux_left[component] + low_speed * (
            star_left[component] - left_state[component]
        )
        right_star_flux = flux_right[component] + high_speed * (
            star_right[component] - right_state[component]
        )
        chosen = jnp.where(high_speed > 0.0, right_star_flux, flux_right[component])
        chosen = jnp.where(middle >= 0.0, left_star_flux, chosen)
        chosen = jnp.where(low_speed >= 0.0, flux_left[component], chosen)
        result.append(chosen)
    return result


def face_fluxes(lower_faces, upper_faces, sweep_axis):
    extent = lower_faces[0].shape[sweep_axis]
    from_below = [window(item, sweep_axis, 0, extent - 1) for item in upper_faces]
    from_above = [window(item, sweep_axis, 1, extent - 1) for item in lower_faces]
    return hllc_flux(from_below, from_above, sweep_axis)


def hydro_step(padded, time_step):
    conserved_list = [padded[component] for component in range(6)]
    extents = padded.shape[1:]
    owned = [extent - 2 * GHOST for extent in extents]
    primitive = primitive_of(conserved_list)
    faces = [traced_faces(primitive, sweep_axis, time_step) for sweep_axis in range(3)]
    predicted = [
        face_fluxes(faces[sweep_axis][0], faces[sweep_axis][1], sweep_axis)
        for sweep_axis in range(3)
    ]
    final_fluxes = []
    for sweep_axis in range(3):
        lower_faces, upper_faces = faces[sweep_axis]
        lower_state = conserved_of(lower_faces)
        upper_state = conserved_of(upper_faces)
        for other_axis in range(3):
            if other_axis != sweep_axis:
                for component in range(6):
                    lower_state[component] = window(
                        lower_state[component], other_axis, GHOST, owned[other_axis]
                    )
                    upper_state[component] = window(
                        upper_state[component], other_axis, GHOST, owned[other_axis]
                    )
        for other_axis in range(3):
            if other_axis != sweep_axis:
                for component in range(6):
                    flux_other = predicted[other_axis][component]
                    divergence = (
                        0.5
                        * time_step
                        * (
                            window(flux_other, other_axis, 1, owned[other_axis])
                            - window(flux_other, other_axis, 0, owned[other_axis])
                        )
                    )
                    for third_axis in range(3):
                        if third_axis == sweep_axis:
                            divergence = window(divergence, third_axis, 3, extents[third_axis] - 6)
                        elif third_axis != other_axis:
                            divergence = window(divergence, third_axis, GHOST, owned[third_axis])
                    lower_state[component] = lower_state[component] - divergence
                    upper_state[component] = upper_state[component] - divergence
        lower_prim = primitive_of(lower_state)
        upper_prim = primitive_of(upper_state)
        final_fluxes.append(face_fluxes(lower_prim, upper_prim, sweep_axis))
    updated = []
    for component in range(6):
        total = conserved_list[component][GHOST:-GHOST, GHOST:-GHOST, GHOST:-GHOST]
        for sweep_axis in range(3):
            flux_here = final_fluxes[sweep_axis][component]
            total = total - time_step * (
                window(flux_here, sweep_axis, 1, owned[sweep_axis])
                - window(flux_here, sweep_axis, 0, owned[sweep_axis])
            )
        updated.append(total)
    return jnp.stack(updated)


def body(conserved_state):
    own_cells = [conserved_state[component] for component in range(6)]
    signal_now = lax.pmax(fastest_signal(own_cells), ("gx", "gy", "gz"))
    time_step = courant / signal_now
    padded = padded_2(conserved_state, (("gz", 3),), GHOST)
    padded = padded_2(padded, (("gy", 2),), GHOST)
    padded = padded_2(padded, (("gx", 1),), GHOST)
    updated = hydro_step(padded, time_step)
    new_cells = [updated[component] for component in range(6)]
    signal_next = lax.pmax(fastest_signal(new_cells), ("gx", "gy", "gz"))
    return (updated, courant / signal_next)


def solution(mesh):
    return jax.shard_map(
        body,
        mesh=mesh,
        in_specs=(P(None, "gx", "gy", "gz"),),
        out_specs=(P(None, "gx", "gy", "gz"), P()),
        check_vma=False,
    )
```

profile of v0, /device:TPU:0, one launch (start us, length us, event | category | flops | bytes accessed | tf_op | source)
XLA Modules:
  0.0 114.1 jit_solution(12096723423511534223)
XLA Ops:
  0.6 1.1 fusion.428
  1.8 3.1 %collective-permute-start = (f32[6,4,8,4]{3,2,1,0:T(8,128)S(1)}, f32[6,4,8,4]{3,2,1,0:T(8,128)S(1)}, u32[]{:S(2)}, u32[]{:S(2)}) collective-permute-start(f32[6,4,8,4]{3,2,1,0:T(8,128)S(1)} %get-tuple-element.267), channel_id=1, source_target_pairs={{0,1},{1,0},{2,3},{3,2},{4,5},{5,4},{6,7},{7,6},{8,9},{9,8},{10,11... | collective-permute-start | bytes 9224 | tf_op jit(solution)/shard_map/ppermute | solution.py:19
  4.9 3.4 %collective-permute-done = f32[6,4,8,4]{3,2,1,0:T(8,128)S(1)} collective-permute-done((f32[6,4,8,4]{3,2,1,0:T(8,128)S(1)}, f32[6,4,8,4]{3,2,1,0:T(8,128)S(1)}, u32[]{:S(2)}, u32[]{:S(2)}) %collective-permute-start) | collective-permute-done | bytes 3104 | tf_op jit(solution)/shard_map/ppermute | solution.py:19
  8.3 1.5 %collective-permute-done.1 = f32[6,4,8,4]{3,2,1,0:T(8,128)S(1)} collective-permute-done((f32[6,4,8,4]{3,2,1,0:T(8,128)S(1)}, f32[6,4,8,4]{3,2,1,0:T(8,128)S(1)}, u32[]{:S(2)}, u32[]{:S(2)}) %collective-permute-start.1) | collective-permute-done | bytes 3104 | tf_op jit(solution)/shard_map/ppermute | solution.py:22
  9.9 1.9 %collective-permute-start.2 = (f32[6,4,4,128]{3,2,1,0:T(4,128)S(1)}, f32[6,4,4,128]{3,2,1,0:T(4,128)S(1)}, u32[]{:S(2)}, u32[]{:S(2)}) collective-permute-start(f32[6,4,4,128]{3,2,1,0:T(4,128)S(1)} %get-tuple-element.265), channel_id=1, source_target_pairs={{0,2},{2,4},{4,6},{6,0},{1,3},{3,5},{5,7},{7,1},{8,10},{10,12},{12... | collective-permute-start | bytes 147464 | tf_op jit(solution)/shard_map/ppermute | solution.py:19
  11.8 2.1 %collective-permute-start.3 = (f32[6,4,4,128]{3,2,1,0:T(4,128)S(1)}, f32[6,4,4,128]{3,2,1,0:T(4,128)S(1)}, u32[]{:S(2)}, u32[]{:S(2)}) collective-permute-start(f32[6,4,4,128]{3,2,1,0:T(4,128)S(1)} %get-tuple-element.266), channel_id=1, source_target_pairs={{2,0},{4,2},{6,4},{0,6},{3,1},{5,3},{7,5},{1,7},{10,8},{12,10},{14... | collective-permute-start | bytes 147464 | tf_op jit(solution)/shard_map/ppermute | solution.py:22
  13.9 2.5 %collective-permute-done.2 = f32[6,4,4,128]{3,2,1,0:T(4,128)S(1)} collective-permute-done((f32[6,4,4,128]{3,2,1,0:T(4,128)S(1)}, f32[6,4,4,128]{3,2,1,0:T(4,128)S(1)}, u32[]{:S(2)}, u32[]{:S(2)}) %collective-permute-start.2) | collective-permute-done | bytes 49184 | tf_op jit(solution)/shard_map/ppermute | solution.py:19
  16.7 0.5 collective-permute-start.4
  17.2 0.6 fusion.341
  17.8 40.1 %pmax.14 = f32[]{:T(128)} all-reduce(f32[]{:T(128)} %fusion.341), channel_id=1, replica_groups=mesh['gx'=4,'gy'=4,'gz'=2] {'gx','gy','gz'}, use_global_device_ids=true, to_apply=%region_1.0 | all-reduce | flops 1 | bytes 8 | tf_op jit(solution)/shard_map/pmax | solution.py:240
  58.6 0.2 pad_maximum_fusion
  59.0 0.2 fusion.75
  60.4 0.2 fusion.63
  60.7 0.3 fusion.28
  61.2 0.3 fusion.57
  62.3 0.4 fusion.129
  62.7 0.3 fusion.410
  62.9 0.2 fusion.416
  63.2 0.2 fusion.419
  63.4 0.3 fusion.23
  63.8 0.3 fusion.19
  64.2 0.4 fusion.11
  65.1 0.3 fusion.397
  65.4 0.2 fusion.403
  65.6 0.3 fusion.401
  66.9 0.2 fusion.213
  67.3 0.3 fusion.21
  67.5 0.3 fusion.9
  67.9 0.3 fusion.13
  70.0 0.7 add_reduce_fusion
  70.7 40.8 %pmax.15 = f32[]{:T(128)} all-reduce(f32[]{:T(128)} %get-tuple-element.2), channel_id=1, replica_groups=mesh['gx'=4,'gy'=4,'gz'=2] {'gx','gy','gz'}, use_global_device_ids=true, to_apply=%region_3.4 | all-reduce | flops 1 | bytes 8 | tf_op jit(solution)/shard_map/pmax | solution.py:247
  112.3 0.6 copy-done.1
  (98 shorter events, 6.3 us)
Async XLA Ops:
  0.6 9.1 %copy-start = (f32[6,4,8,120]{3,2,1,0:T(8,128)S(1)}, f32[6,4,8,120]{3,2,1,0:T(8,128)}, u32[]{:S(2)}) copy-start(f32[6,4,8,120]{3,2,1,0:T(8,128)} %param.1) | copy-start | bytes 276484
  1.8 6.5 %collective-permute-start = (f32[6,4,8,4]{3,2,1,0:T(8,128)S(1)}, f32[6,4,8,4]{3,2,1,0:T(8,128)S(1)}, u32[]{:S(2)}, u32[]{:S(2)}) collective-permute-start(f32[6,4,8,4]{3,2,1,0:T(8,128)S(1)} %get-tuple-element.267), channel_id=1, source_target_pairs={{0,1},{1,0},{2,3},{3,2},{4,5},{5,4},{6,7},{7,6},{8,9},{9,8},{10,11... | collective-permute-start | bytes 9224 | tf_op jit(solution)/shard_map/ppermute | solution.py:19
  4.8 4.9 %collective-permute-start.1 = (f32[6,4,8,4]{3,2,1,0:T(8,128)S(1)}, f32[6,4,8,4]{3,2,1,0:T(8,128)S(1)}, u32[]{:S(2)}, u32[]{:S(2)}) collective-permute-start(f32[6,4,8,4]{3,2,1,0:T(8,128)S(1)} %get-tuple-element.268), channel_id=1, source_target_pairs={{1,0},{0,1},{3,2},{2,3},{5,4},{4,5},{7,6},{6,7},{9,8},{8,9},{11,10... | collective-permute-start | bytes 9224 | tf_op jit(solution)/shard_map/ppermute | solution.py:22
  9.9 6.5 %collective-permute-start.2 = (f32[6,4,4,128]{3,2,1,0:T(4,128)S(1)}, f32[6,4,4,128]{3,2,1,0:T(4,128)S(1)}, u32[]{:S(2)}, u32[]{:S(2)}) collective-permute-start(f32[6,4,4,128]{3,2,1,0:T(4,128)S(1)} %get-tuple-element.265), channel_id=1, source_target_pairs={{0,2},{2,4},{4,6},{6,0},{1,3},{3,5},{5,7},{7,1},{8,10},{10,12},{12... | collective-permute-start | bytes 147464 | tf_op jit(solution)/shard_map/ppermute | solution.py:19
  11.8 4.6 %collective-permute-start.3 = (f32[6,4,4,128]{3,2,1,0:T(4,128)S(1)}, f32[6,4,4,128]{3,2,1,0:T(4,128)S(1)}, u32[]{:S(2)}, u32[]{:S(2)}) collective-permute-start(f32[6,4,4,128]{3,2,1,0:T(4,128)S(1)} %get-tuple-element.266), channel_id=1, source_target_pairs={{2,0},{4,2},{6,4},{0,6},{3,1},{5,3},{7,5},{1,7},{10,8},{12,10},{14... | collective-permute-start | bytes 147464 | tf_op jit(solution)/shard_map/ppermute | solution.py:22
  16.6 42.0 %collective-permute-start.5 = (f32[6,4,16,128]{3,2,1,0:T(8,128)S(1)}, f32[6,4,16,128]{3,2,1,0:T(8,128)S(1)}, u32[]{:S(2)}, u32[]{:S(2)}) collective-permute-start(f32[6,4,16,128]{3,2,1,0:T(8,128)S(1)} %pad_maximum_fusion.1), channel_id=1, source_target_pairs={{8,0},{16,8},{24,16},{0,24},{9,1},{17,9},{25,17},{1,25},{10,2},{18... | collective-permute-start | bytes 589832 | tf_op jit(solution)/shard_map/ppermute | solution.py:22
  16.7 42.0 %collective-permute-start.4 = (f32[6,4,16,128]{3,2,1,0:T(8,128)S(1)}, f32[6,4,16,128]{3,2,1,0:T(8,128)S(1)}, u32[]{:S(2)}, u32[]{:S(2)}) collective-permute-start(f32[6,4,16,128]{3,2,1,0:T(8,128)S(1)} %pad_maximum_fusion.1), channel_id=1, source_target_pairs={{0,8},{8,16},{16,24},{24,0},{1,9},{9,17},{17,25},{25,1},{2,10},{10... | collective-permute-start | bytes 589832 | tf_op jit(solution)/shard_map/ppermute | solution.py:19
  112.3 0.6 copy-start.1
where the time goes:
time: 115 us; the launch traced here: 114 us
  blocking collectives  80.9 us (70%)
  other arithmetic  11.3 us (10%)
  starting transfers between devices  7.71 us (7%)
  waiting for transfers between devices  7.35 us (6%)
  between operations  3.82 us (3%)
  local copies, waits for them, and re-layouts  3.07 us (3%)
    pmax x1, blocking collectives, body(): signal_next = lax.pmax(fastest_signal(new_cells), ('gx', 'gy', 'gz'))  40.8 us
    pmax x1, blocking collectives, body(): signal_now = lax.pmax(fastest_signal(own_cells), ('gx', 'gy', 'gz'))  40.1 us
    ppermute x3, waiting for transfers between devices, padded_2(): lax.ppermute(lax.slice_in_dim(block, block.shape[dim] - width, None, axis...  5.89 us
    ppermute x3, starting transfers between devices, padded_2(): lax.ppermute(lax.slice_in_dim(block, block.shape[dim] - width, None, axis...  5.49 us
    select_n x18, other arithmetic, hllc_flux(): chosen = jnp.where(low_speed >= 0.0, flux_left[component], chosen)  3.19 us
  transfers between devices with their start and end apart: 6, of which 3 were waited for; matrix products, arithmetic and copies ran while one was open for 1% of the time, Pallas kernels for 0%

commit v1 on v0

v1 whole, which is shorter than its diff:
```python
import functools

import jax
import jax.numpy as jnp
from jax import lax
from jax.experimental import pallas as pl
from jax.experimental.pallas import tpu as pltpu
from jax.sharding import PartitionSpec as P

GHOST = 4
ROWS = 8
LANES = 128
COMPS = 6

adiabatic = 5.0 / 3.0
courant = 0.3
MESH_ID = pl.DeviceIdType.MESH


def primitive_of(u):
    inverse = 1.0 / u[0]
    velocity = [u[component] * inverse for component in (1, 2, 3)]
    kinetic = 0.5 * (u[1] * velocity[0] + u[2] * velocity[1] + u[3] * velocity[2])
    pressure = (adiabatic - 1.0) * (u[4] - kinetic)
    return [u[0], velocity[0], velocity[1], velocity[2], pressure, u[5] * inverse]


def conserved_of(q):
    density = q[0]
    momenta = [density * q[component] for component in (1, 2, 3)]
    kinetic = 0.5 * (momenta[0] * q[1] + momenta[1] * q[2] + momenta[2] * q[3])
    energy = q[4] * (1.0 / (adiabatic - 1.0)) + kinetic
    return [density, momenta[0], momenta[1], momenta[2], energy, density * q[5]]


def signal_of(u):
    q = primitive_of(u)
    sound = jnp.sqrt(adiabatic * q[4] / q[0])
    return jnp.maximum(jnp.maximum(jnp.abs(q[1]), jnp.abs(q[2])), jnp.abs(q[3])) + sound


def edge_of(b3, b2, b1, c, a1, a2):
    edge = (37.0 * (b1 + c) - 8.0 * (b2 + a1) + (b3 + a2)) * (1.0 / 60.0)
    return jnp.minimum(jnp.maximum(edge, jnp.minimum(b1, c)), jnp.maximum(b1, c))


def limited(lower, upper, centre):
    flatten = (upper - centre) * (centre - lower) <= 0.0
    spread = upper - lower
    skewed = spread * (centre - 0.5 * (lower + upper))
    limit = spread * spread * (1.0 / 6.0)
    new_lower = jnp.where(skewed > limit, 3.0 * centre - 2.0 * upper, lower)
    new_upper = jnp.where(skewed < -limit, 3.0 * centre - 2.0 * lower, upper)
    return jnp.where(flatten, centre, new_lower), jnp.where(flatten, centre, new_upper)


def traced(q, edges, axis, half):
    normal = 1 + axis
    slopes = [pair[1] - pair[0] for pair in edges]
    n = q[normal] * half
    rates = []
    for component in range(COMPS):
        rate = n * slopes[component]
        if component == 0:
            rate = rate + (q[0] * half) * slopes[normal]
        elif component == normal:
            rate = rate + (half / q[0]) * slopes[4]
        elif component == 4:
            rate = rate + (adiabatic * half) * q[4] * slopes[normal]
        rates.append(rate)
    lower = [edges[component][0] - rates[component] for component in range(COMPS)]
    upper = [edges[component][1] - rates[component] for component in range(COMPS)]
    return lower, upper


def hllc(left, right, axis):
    normal = 1 + axis
    t1, t2 = [component for component in (1, 2, 3) if component != normal]
    ratio_l = left[4] / left[0]
    ratio_r = right[4] / right[0]
    sound_l = jnp.sqrt(adiabatic * ratio_l)
    sound_r = jnp.sqrt(adiabatic * ratio_r)
    n_l, n_r = left[normal], right[normal]
    low = jnp.minimum(n_l - sound_l, n_r - sound_r)
    high = jnp.maximum(n_l + sound_l, n_r + sound_r)
    mass_l = left[0] * (low - n_l)
    mass_r = right[0] * (high - n_r)
    middle = (right[4] - left[4] + mass_l * n_l - mass_r * n_r) / (mass_l - mass_r)
    on_left = middle >= 0.0
    pick = lambda a, b: jnp.where(on_left, a, b)
    r, n, p = pick(left[0], right[0]), pick(n_l, n_r), pick(left[4], right[4])
    v, w, tracer = pick(left[t1], right[t1]), pick(left[t2], right[t2]), pick(left[5], right[5])
    ratio, mass = pick(ratio_l, ratio_r), pick(mass_l, mass_r)
    outer = pick(low, high)
    speed = pick(jnp.minimum(low, 0.0), jnp.maximum(high, 0.0))
    factor = mass / (outer - middle)
    flux = r * n + speed * (factor - r)
    gain = speed * factor * (middle - n)
    energy = ratio * (1.0 / (adiabatic - 1.0)) + 0.5 * (n * n + v * v + w * w)
    result = [None] * COMPS
    result[0] = flux
    result[normal] = n * flux + p + gain
    result[t1] = v * flux
    result[t2] = w * flux
    result[4] = energy * flux + n * p + gain * (middle + p / mass)
    result[5] = tracer * flux
    return result


def rolled(x, offset, axis):
    return pltpu.roll(x, (-offset) % x.shape[axis], axis)


def kernel(sizes, u_hbm, out_ref, next_ref, own, rx, ysend, ry, y1send, zsend, rz, rxy, rxy1, u, q,
           face, pred, msend, mrecv, own_sem, send_sem, recv_sem, msend_sem, mrecv_sem):
    nx, ny, nz = sizes
    devices = nx * ny * nz
    comps, cx, cy, cz = own.shape
    slots = LANES // GHOST
    ix, iy, iz = lax.axis_index("gx"), lax.axis_index("gy"), lax.axis_index("gz")
    me = (ix * ny + iy) * nz + iz

    load = pltpu.make_async_copy(u_hbm, own, own_sem)
    load.start()

    def place(k):
        target = lax.rem(me + k, devices)
        return (lax.div(target, ny * nz), lax.rem(lax.div(target, nz), ny), lax.rem(target, nz))

    barrier = pltpu.get_barrier_semaphore()

    def greet(k, carry):
        pl.semaphore_signal(barrier, inc=1, device_id=place(k), device_id_type=MESH_ID)
        return carry

    lax.fori_loop(1, devices, greet, 0)
    load.wait()

    lane = lax.broadcasted_iota(jnp.int32, (ROWS, LANES), 1)
    row = lax.broadcasted_iota(jnp.int32, (ROWS, LANES), 0)
    upper_half = row < GHOST
    zero_tail = jnp.zeros((ROWS, LANES - cz), jnp.float32)

    def body(ref, c, x):
        return jnp.concatenate([ref[c, x], zero_tail], axis=1)

    tiles = [[body(own, c, x) for x in range(cx)] for c in range(COMPS)]
    best = None
    for x in range(cx):
        speeds = signal_of([tiles[c][x] for c in range(COMPS)])
        best = speeds if best is None else jnp.maximum(best, speeds)
    best = jnp.max(jnp.where(lane < cz, best, 0.0), axis=0, keepdims=True)
    msend[0] = best
    packs = [[None, None] for _ in range(zsend.shape[1])]
    for c in range(COMPS):
        for x in range(cx):
            slot = c * cx + x
            block, at = slot // slots, slot % slots * GHOST
            inside = (lane >= at) & (lane < at + GHOST)
            for side in range(2):
                start = 0 if side == 0 else cz - GHOST
                moved = pltpu.roll(tiles[c][x], (at - start) % LANES, 1)
                held = packs[block][side]
                packs[block][side] = moved if held is None else jnp.where(inside, moved, held)
    for block in range(zsend.shape[1]):
        for side in range(2):
            zsend[side, block] = packs[block][side]
    for x in range(cx):
        for pair in range(COMPS // 2):
            first, second = tiles[2 * pair][x], tiles[2 * pair + 1][x]
            swapped = pltpu.roll(second, GHOST, 0)
            ysend[0, x, pair] = jnp.where(upper_half, first, swapped)
            ysend[1, x, pair] = jnp.where(upper_half, swapped, first)
        for c in range(COMPS):
            y1send[0, x, c : c + 1] = tiles[c][x][0:1]
            y1send[1, x, c : c + 1] = tiles[c][x][ROWS - 1 : ROWS]

    pl.semaphore_wait(barrier, devices - 1)

    copies = []

    def send(src, dst, dx, dy, dz):
        number = len(copies)
        copy = pltpu.make_async_remote_copy(
            src_ref=src, dst_ref=dst, send_sem=send_sem.at[number], recv_sem=recv_sem.at[number],
            device_id=(lax.rem(ix + dx + nx, nx), lax.rem(iy + dy + ny, ny), lax.rem(iz + dz + nz, nz)),
            device_id_type=MESH_ID)
        copy.start()
        copies.append(copy)

    for dx in (-1, 1):
        send(own, rx.at[(1 - dx) // 2], dx, 0, 0)

    def share(turn):
        def one(k, carry):
            pltpu.make_async_remote_copy(
                src_ref=msend.at[turn], dst_ref=mrecv.at[turn, k - 1], send_sem=msend_sem.at[turn],
                recv_sem=mrecv_sem.at[turn], device_id=place(k), device_id_type=MESH_ID).start()
            return carry
        lax.fori_loop(1, devices, one, 0)

    def gather(turn):
        pltpu.make_async_copy(mrecv.at[turn], mrecv.at[turn], mrecv_sem.at[turn]).wait()
        pltpu.make_async_copy(mrecv.at[turn], mrecv.at[turn], msend_sem.at[turn]).wait()
        return jnp.maximum(jnp.max(mrecv[turn], axis=0), msend[turn])

    for dy in (-1, 1):
        side = (dy + 1) // 2
        for dx in (-1, 1):
            corner = (1 - dx) // 2 * 2 + 1 - side
            plane = 0 if dx == -1 else cx - 1
            send(ysend.at[side, plane], rxy.at[corner], dx, dy, 0)
            send(y1send.at[side], rxy1.at[corner], dx, dy, 0)
        send(ysend.at[side], ry.at[1 - side], 0, dy, 0)
    for dz in (-1, 1):
        side = (dz + 1) // 2
        for dx in (-1, 0, 1):
            for dy in (-1, 0, 1):
                send(zsend.at[side], rz.at[1 - dx, 1 - dy, 1 - side], dx, dy, dz)
    share(0)

    for copy in copies:
        copy.wait()

    in_body = lane < cz
    in_high = lane < cz + GHOST

    def ghosted(tile, high, low, c, x):
        slot = c * cx + x
        block, at = slot // slots, slot % slots * GHOST
        up = pltpu.roll(high[block], (cz - at) % LANES, 1)
        down = pltpu.roll(low[block], (LANES - GHOST - at) % LANES, 1)
        return jnp.where(in_body, tile, jnp.where(in_high, up, down))

    blocks = range(zsend.shape[1])
    for dx in range(3):
        plain = [[rz[dx, 1, side, block] for block in blocks] for side in (1, 0)]
        mixed = [[jnp.where(upper_half, rz[dx, 2, side, block], rz[dx, 0, side, block]) for block in blocks]
                 for side in (1, 0)]
        for x in range(cx):
            at = dx * cx + x
            near = dx == 1 or (dx == 0 and x == cx - 1) or (dx == 2 and x == 0)
            side_tiles = []
            if near:
                for pair in range(COMPS // 2):
                    if dx == 1:
                        below, above = ry[0, x, pair], ry[1, x, pair]
                    else:
                        below, above = rxy[dx // 2 * 2, pair], rxy[dx // 2 * 2 + 1, pair]
                    side_tiles.append(jnp.where(upper_half, above, below))
                    side_tiles.append(pltpu.roll(jnp.where(upper_half, below, above), GHOST, 0))
            else:
                below, above = rxy1[dx // 2 * 2, x], rxy1[dx // 2 * 2 + 1, x]
                for c in range(COMPS):
                    side_tiles.append(jnp.where(upper_half, pltpu.roll(above, (-c) % ROWS, 0),
                                                pltpu.roll(below, (ROWS - 1 - c) % ROWS, 0)))
            state_a, state_b = [], []
            for c in range(COMPS):
                tile = tiles[c][x] if dx == 1 else body(rx.at[dx // 2], c, x)
                state_a.append(ghosted(tile, plain[0], plain[1], c, x))
                state_b.append(ghosted(side_tiles[c], mixed[0], mixed[1], c, x))
            prim_a, prim_b = primitive_of(state_a), primitive_of(state_b)
            for c in range(COMPS):
                if dx == 1:
                    u[c, x] = state_a[c]
                q[c, at, 0:ROWS] = prim_a[c]
                q[c, at, ROWS:] = prim_b[c]

    now = gather(0)
    dt = courant / jnp.max(now, axis=1, keepdims=True)
    step = jnp.broadcast_to(dt, (2 * ROWS, LANES))
    half = 0.5 * step

    base = cx - 1
    count = cx + 2
    for i in range(count):
        at = base + i
        centre = [q[c, at] for c in range(COMPS)]
        for axis in range(3):
            edges = []
            for c in range(COMPS):
                if axis == 0:
                    near = [q[c, at + offset] for offset in (-3, -2, -1, 0, 1, 2, 3)]
                    lower = edge_of(*near[:6])
                    upper = edge_of(*near[1:])
                else:
                    near = [rolled(centre[c], offset, axis - 1) if offset else centre[c]
                            for offset in (-3, -2, -1, 0, 1, 2)]
                    lower = edge_of(*near)
                    upper = rolled(lower, 1, axis - 1)
                edges.append(limited(lower, upper, centre[c]))
            lower_faces, upper_faces = traced(centre, edges, axis, half)
            for c in range(COMPS):
                face[axis, 0, c, i] = lower_faces[c]
                face[axis, 1, c, i] = upper_faces[c]

    for i in range(count):
        for axis in range(3):
            if axis == 0 and i == 0:
                continue
            right = [face[axis, 0, c, i] for c in range(COMPS)]
            if axis == 0:
                left = [face[0, 1, c, i - 1] for c in range(COMPS)]
            else:
                left = [rolled(face[axis, 1, c, i], -1, axis - 1) for c in range(COMPS)]
            flux = hllc(left, right, axis)
            for c in range(COMPS):
                pred[axis, c, i] = flux[c] * half

    def differ(axis, c, i, rows):
        if axis == 0:
            return pred[0, c, i + 1, 0:rows] - pred[0, c, i, 0:rows]
        flux = pred[axis, c, i]
        return (rolled(flux, 1, axis - 1) - flux)[0:rows]

    def corrected(axis, i, rows):
        others = [other for other in range(3) if other != axis]
        change = [differ(others[0], c, i, rows) + differ(others[1], c, i, rows) for c in range(COMPS)]
        result = []
        for side in range(2):
            state = conserved_of([face[axis, side, c, i, 0:rows] for c in range(COMPS)])
            result.append(primitive_of([state[c] - change[c] for c in range(COMPS)]))
        return result

    total = [[u[c, x] for c in range(COMPS)] for x in range(cx)]
    thin = step[0:ROWS]
    before = corrected(0, 0, ROWS)
    flux_before = None
    for i in range(1, count):
        after = corrected(0, i, ROWS)
        flux = hllc(before[1], after[0], 0)
        if flux_before is not None:
            x = i - 2
            total[x] = [total[x][c] - thin * (flux[c] - flux_before[c]) for c in range(COMPS)]
        before, flux_before = after, flux
    best = None
    for x in range(cx):
        lower, upper = corrected(1, x + 1, 2 * ROWS)
        flux = hllc([rolled(item, -1, 0) for item in upper], lower, 1)
        total[x] = [total[x][c] - thin * (rolled(flux[c], 1, 0) - flux[c])[0:ROWS] for c in range(COMPS)]
        lower, upper = corrected(2, x + 1, ROWS)
        flux = hllc([rolled(item, -1, 1) for item in upper], lower, 2)
        total[x] = [total[x][c] - thin * (rolled(flux[c], 1, 1) - flux[c]) for c in range(COMPS)]
        for c in range(COMPS):
            out_ref[c, x] = total[x][c][:, 0:cz]
        speeds = signal_of(total[x])
        best = speeds if best is None else jnp.maximum(best, speeds)
    msend[1] = jnp.max(jnp.where(in_body, best, 0.0), axis=0, keepdims=True)
    share(1)
    next_ref[0, 0] = courant / jnp.max(gather(1))


def body(sizes, conserved_state):
    comps, cx, cy, cz = conserved_state.shape
    assert comps == COMPS and cx == GHOST and cy == ROWS and cz + 2 * GHOST <= LANES
    devices = sizes[0] * sizes[1] * sizes[2]
    blocks = -(-COMPS * cx * GHOST // LANES)
    f32 = jnp.float32
    vmem = lambda *shape: pltpu.VMEM(shape, f32)
    pairs = COMPS // 2
    messages = 2 + 8 + 2 + 18
    updated, following = pl.pallas_call(
        functools.partial(kernel, sizes),
        out_shape=(jax.ShapeDtypeStruct(conserved_state.shape, f32), jax.ShapeDtypeStruct((1, 1), f32)),
        in_specs=[pl.BlockSpec(memory_space=pl.ANY)],
        out_specs=(pl.BlockSpec(memory_space=pltpu.VMEM), pl.BlockSpec(memory_space=pltpu.SMEM)),
        scratch_shapes=[
            vmem(COMPS, cx, cy, cz),
            vmem(2, COMPS, cx, cy, cz),
            vmem(2, cx, pairs, ROWS, LANES),
            vmem(2, cx, pairs, ROWS, LANES),
            vmem(2, cx, ROWS, LANES),
            vmem(2, blocks, ROWS, LANES),
            vmem(3, 3, 2, blocks, ROWS, LANES),
            vmem(4, pairs, ROWS, LANES),
            vmem(4, cx, ROWS, LANES),
            vmem(COMPS, cx, ROWS, LANES),
            vmem(COMPS, 3 * cx, 2 * ROWS, LANES),
            vmem(3, 2, COMPS, cx + 2, 2 * ROWS, LANES),
            vmem(3, COMPS, cx + 2, 2 * ROWS, LANES),
            vmem(2, 1, LANES),
            vmem(2, devices - 1, 1, LANES),
            pltpu.SemaphoreType.DMA,
            pltpu.SemaphoreType.DMA((messages,)),
            pltpu.SemaphoreType.DMA((messages,)),
            pltpu.SemaphoreType.DMA((2,)),
            pltpu.SemaphoreType.DMA((2,)),
        ],
        compiler_params=pltpu.CompilerParams(collective_id=0, has_side_effects=True),
    )(conserved_state)
    return updated, following.reshape(())


def solution(mesh):
    sizes = tuple(mesh.shape[axis] for axis in ("gx", "gy", "gz"))
    return jax.shard_map(
        functools.partial(body, sizes),
        mesh=mesh,
        in_specs=(P(None, "gx", "gy", "gz"),),
        out_specs=(P(None, "gx", "gy", "gz"), P()),
        check_vma=False,
    )
```

time: 115 us -> 29.8 us (0.26)
  blocking collectives: 80.9 us -> 0 us
  Pallas kernels: 0 us -> 25.6 us
  other arithmetic: 11.3 us -> 0 us
  starting transfers between devices: 7.71 us -> 0 us
  waiting for transfers between devices: 7.35 us -> 0 us
  local copies, waits for them, and re-layouts: 3.07 us -> 1.54 us
  between operations: 3.82 us -> 2.46 us
    pmax x2 -> x0, blocking collectives: 80.9 us -> none  [the longest x1 40.8 us: body(): signal_next = lax.pmax(fastest_signal(new_cells), ('gx', 'gy', 'gz'))]
    pallas_call x0 -> x1, Pallas kernels: none -> 25.6 us  [body(): pl.pallas_call(functools.partial(kernel, sizes), out_shape=(jax.ShapeDtyp...]
    ppermute x6 -> x0, starting transfers between devices: 7.71 us -> none  [the longest x3 5.49 us: padded_2(): lax.ppermute(lax.slice_in_dim(block, block.shape[dim] - width, None, axis...]
    ppermute x6 -> x0, waiting for transfers between devices: 7.35 us -> none  [the longest x3 5.89 us: padded_2(): lax.ppermute(lax.slice_in_dim(block, block.shape[dim] - width, None, axis...]
    mul x37 -> x0, other arithmetic: 3.45 us -> none  [the longest x10 1.82 us: conserved_of(): momenta = [density * primitive[component] for component in (1, 2, 3)]]
    select_n x18 -> x0, other arithmetic: 3.19 us -> none  [hllc_flux(): chosen = jnp.where(low_speed >= 0.0, flux_left[component], chosen)]
    slice x26 -> x0, local copies, waits for them, and re-layouts: 2.37 us -> none  [the longest x24 1.23 us: window(): return lax.slice_in_dim(values, start, start + length, axis=axis_number)]
    min x11 -> x0, other arithmetic: 1.79 us -> none  [parabola(): jnp.clip(edge, jnp.minimum(before_one, middle), jnp.maximum(before_one, m...]
  transfers between devices with their start and end apart: 6 -> 0, of which waited for: 3 -> 0; matrix products, arithmetic and copies ran while one was open for 1% -> 0% of each run, Pallas kernels for 0% -> 0%
where the time goes in v1:
time: 29.8 us; the launch traced here: 29.6 us
  Pallas kernels  25.6 us (86%)
  between operations  2.46 us (8%)
  local copies, waits for them, and re-layouts  1.54 us (5%)
    pallas_call x1, Pallas kernels, body(): pl.pallas_call(functools.partial(kernel, sizes), out_shape=(jax.ShapeDtyp...  25.6 us
    unnamed x1, local copies, waits for them, and re-layouts  1.54 us

profile of v1, /device:TPU:0, one launch (start us, length us, event | category | flops | bytes accessed | tf_op | source)
XLA Modules:
  0.0 29.6 jit_solution(18410071545081143307)
XLA Ops:
  0.6 25.6 %shard_map.30 = (f32[6,4,8,120]{3,2,1,0:T(8,128)}, f32[1,1]{1,0:T(1,128)}) custom-call(f32[6,4,8,120]{3,2,1,0:T(8,128)} %u_hbm.1), custom_call_target="tpu_custom_call" | custom-call | tf_op jit(solution)/shard_map/pallas_call | solution.py:362
  26.2 1.5 %copy.5 = f32[6,4,8,120]{3,2,1,0:T(8,128)} copy(f32[6,4,8,120]{3,2,1,0:T(8,128)} %get-tuple-element.8) | data formatting | bytes 184320

commit v2 on v1

--- a/solution.py
+++ b/solution.py
@@ -9,6 +9,7 @@
 
 GHOST = 4
 ROWS = 8
+UNROLL = 64
 LANES = 128
 COMPS = 6
 
@@ -129,11 +130,25 @@
 
     barrier = pltpu.get_barrier_semaphore()
 
-    def greet(k, carry):
-        pl.semaphore_signal(barrier, inc=1, device_id=place(k), device_id_type=MESH_ID)
-        return carry
-
-    lax.fori_loop(1, devices, greet, 0)
+    def wrap(value, size):
+        return jnp.where(value >= size, value - size, value)
+
+    coordinates = [[wrap(index + k, size) for k in range(size)] if devices <= UNROLL else None
+                   for index, size in ((ix, nx), (iy, ny), (iz, nz))]
+
+    def everyone(act):
+        if devices > UNROLL:
+            def one(k, carry):
+                act(k - 1, place(k))
+                return carry
+            lax.fori_loop(1, devices, one, 0)
+            return
+        far = [(min(kx, nx - kx) + min(ky, ny - ky) + min(kz, nz - kz), kx, ky, kz)
+               for kx in range(nx) for ky in range(ny) for kz in range(nz)]
+        for _, kx, ky, kz in sorted(far, reverse=True)[:-1]:
+            act((kx * ny + ky) * nz + kz - 1, (coordinates[0][kx], coordinates[1][ky], coordinates[2][kz]))
+
+    everyone(lambda slot, device: pl.semaphore_signal(barrier, inc=1, device_id=device, device_id_type=MESH_ID))
     load.wait()
 
     lane = lax.broadcasted_iota(jnp.int32, (ROWS, LANES), 1)
@@ -178,6 +193,7 @@
     pl.semaphore_wait(barrier, devices - 1)
 
     copies = []
+    early, late = [], []
 
     def send(src, dst, dx, dy, dz):
         number = len(copies)
@@ -187,17 +203,18 @@
             device_id_type=MESH_ID)
         copy.start()
         copies.append(copy)
+        if dx:
+            late.append(copy)
+        else:
+            early.append(copy)
 
     for dx in (-1, 1):
         send(own, rx.at[(1 - dx) // 2], dx, 0, 0)
 
     def share(turn):
-        def one(k, carry):
-            pltpu.make_async_remote_copy(
-                src_ref=msend.at[turn], dst_ref=mrecv.at[turn, k - 1], send_sem=msend_sem.at[turn],
-                recv_sem=mrecv_sem.at[turn], device_id=place(k), device_id_type=MESH_ID).start()
-            return carry
-        lax.fori_loop(1, devices, one, 0)
+        everyone(lambda slot, device: pltpu.make_async_remote_copy(
+            src_ref=msend.at[turn], dst_ref=mrecv.at[turn, slot], send_sem=msend_sem.at[turn],
+            recv_sem=mrecv_sem.at[turn], device_id=device, device_id_type=MESH_ID).start())
 
     def gather(turn):
         pltpu.make_async_copy(mrecv.at[turn], mrecv.at[turn], mrecv_sem.at[turn]).wait()
@@ -219,8 +236,8 @@
                 send(zsend.at[side], rz.at[1 - dx, 1 - dy, 1 - side], dx, dy, dz)
     share(0)
 
-    for copy in copies:
-        copy.wait()
+    for copy in early:
+        copy.wait_recv()
 
     in_body = lane < cz
     in_high = lane < cz + GHOST
@@ -233,7 +250,7 @@
         return jnp.where(in_body, tile, jnp.where(in_high, up, down))
 
     blocks = range(zsend.shape[1])
-    for dx in range(3):
+    def assemble(dx):
         plain = [[rz[dx, 1, side, block] for block in blocks] for side in (1, 0)]
         mixed = [[jnp.where(upper_half, rz[dx, 2, side, block], rz[dx, 0, side, block]) for block in blocks]
                  for side in (1, 0)]
@@ -266,6 +283,36 @@
                 q[c, at, 0:ROWS] = prim_a[c]
                 q[c, at, ROWS:] = prim_b[c]
 
+    def trace(axis, i):
+        at = base + i
+        centre = [q[c, at] for c in range(COMPS)]
+        edges = []
+        for c in range(COMPS):
+            if axis == 0:
+                near = [q[c, at + offset] for offset in (-3, -2, -1, 0, 1, 2, 3)]
+                lower = edge_of(*near[:6])
+                upper = edge_of(*near[1:])
+            else:
+                near = [rolled(centre[c], offset, axis - 1) if offset else centre[c]
+                        for offset in (-3, -2, -1, 0, 1, 2)]
+                lower = edge_of(*near)
+                upper = rolled(lower, 1, axis - 1)
+            edges.append(limited(lower, upper, centre[c]))
+        lower_faces, upper_faces = traced(centre, edges, axis, half)
+        for c in range(COMPS):
+            face[axis, 0, c, i] = lower_faces[c]
+            face[axis, 1, c, i] = upper_faces[c]
+        if axis:
+            predict(axis, i, [rolled(item, -1, axis - 1) for item in upper_faces], lower_faces)
+        elif i:
+            predict(axis, i, [face[0, 1, c, i - 1] for c in range(COMPS)], lower_faces)
+
+    def predict(axis, i, left, right):
+        flux = hllc(left, right, axis)
+        for c in range(COMPS):
+            pred[axis, c, i] = flux[c] * half
+
+    assemble(1)
     now = gather(0)
     dt = courant / jnp.max(now, axis=1, keepdims=True)
     step = jnp.broadcast_to(dt, (2 * ROWS, LANES))
@@ -273,39 +320,18 @@
 
     base = cx - 1
     count = cx + 2
+    for i in range(1, count - 1):
+        for axis in (1, 2):
+            trace(axis, i)
+    for copy in late:
+        copy.wait_recv()
+    assemble(0)
+    assemble(2)
     for i in range(count):
-        at = base + i
-        centre = [q[c, at] for c in range(COMPS)]
-        for axis in range(3):
-            edges = []
-            for c in range(COMPS):
-                if axis == 0:
-                    near = [q[c, at + offset] for offset in (-3, -2, -1, 0, 1, 2, 3)]
-                    lower = edge_of(*near[:6])
-                    upper = edge_of(*near[1:])
-                else:
-                    near = [rolled(centre[c], offset, axis - 1) if offset else centre[c]
-                            for offset in (-3, -2, -1, 0, 1, 2)]
-                    lower = edge_of(*near)
-                    upper = rolled(lower, 1, axis - 1)
-                edges.append(limited(lower, upper, centre[c]))
-            lower_faces, upper_faces = traced(centre, edges, axis, half)
-            for c in range(COMPS):
-                face[axis, 0, c, i] = lower_faces[c]
-                face[axis, 1, c, i] = upper_faces[c]
-
-    for i in range(count):
-        for axis in range(3):
-            if axis == 0 and i == 0:
-                continue
-            right = [face[axis, 0, c, i] for c in range(COMPS)]
-            if axis == 0:
-                left = [face[0, 1, c, i - 1] for c in range(COMPS)]
-            else:
-                left = [rolled(face[axis, 1, c, i], -1, axis - 1) for c in range(COMPS)]
-            flux = hllc(left, right, axis)
-            for c in range(COMPS):
-                pred[axis, c, i] = flux[c] * half
+        trace(0, i)
+        if i == 0 or i == count - 1:
+            trace(1, i)
+            trace(2, i)
 
     def differ(axis, c, i, rows):
         if axis == 0:
@@ -347,6 +373,8 @@
         best = speeds if best is None else jnp.maximum(best, speeds)
     msend[1] = jnp.max(jnp.where(in_body, best, 0.0), axis=0, keepdims=True)
     share(1)
+    for copy in copies:
+        copy.wait_send()
     next_ref[0, 0] = courant / jnp.max(gather(1))
 
 

time: 29.8 us -> 29.3 us (0.983)
  Pallas kernels: 25.6 us -> 25.2 us
    pallas_call x1, Pallas kernels: 25.6 us -> 25.2 us  [body(): pl.pallas_call(functools.partial(kernel, sizes), out_shape=(jax.ShapeDtyp...]
where the time goes in v2:
time: 29.3 us; the launch traced here: 29.2 us
  Pallas kernels  25.2 us (86%)
  between operations  2.46 us (8%)
  local copies, waits for them, and re-layouts  1.54 us (5%)
    pallas_call x1, Pallas kernels, body(): pl.pallas_call(functools.partial(kernel, sizes), out_shape=(jax.ShapeDtyp...  25.2 us
    unnamed x1, local copies, waits for them, and re-layouts  1.54 us

profile of v2, /device:TPU:0, one launch (start us, length us, event | category | flops | bytes accessed | tf_op | source)
XLA Modules:
  0.0 29.2 jit_solution(9313236441193145319)
XLA Ops:
  0.6 25.2 %shard_map.30 = (f32[6,4,8,120]{3,2,1,0:T(8,128)}, f32[1,1]{1,0:T(1,128)}) custom-call(f32[6,4,8,120]{3,2,1,0:T(8,128)} %u_hbm.1), custom_call_target="tpu_custom_call" | custom-call | tf_op jit(solution)/shard_map/pallas_call | solution.py:390
  25.8 1.5 %copy.5 = f32[6,4,8,120]{3,2,1,0:T(8,128)} copy(f32[6,4,8,120]{3,2,1,0:T(8,128)} %get-tuple-element.8) | data formatting | bytes 184320

commit v3 on v2

--- a/solution.py
+++ b/solution.py
@@ -9,7 +9,6 @@
 
 GHOST = 4
 ROWS = 8
-UNROLL = 64
 LANES = 128
 COMPS = 6
 
@@ -112,43 +111,35 @@
     return pltpu.roll(x, (-offset) % x.shape[axis], axis)
 
 
-def kernel(sizes, u_hbm, out_ref, next_ref, own, rx, ysend, ry, y1send, zsend, rz, rxy, rxy1, u, q,
-           face, pred, msend, mrecv, own_sem, send_sem, recv_sem, msend_sem, mrecv_sem):
+def kernel(sizes, u_hbm, out_ref, next_ref, own, rx, ysend, ry, corner_send, zsend, rz, rxy, u, q,
+           face, pred, msend, mrecv_x, mrecv_yz, own_sem, send_sem, recv_sem, msend_sem, mrecv_sem):
     nx, ny, nz = sizes
-    devices = nx * ny * nz
     comps, cx, cy, cz = own.shape
     slots = LANES // GHOST
+    mrecv = (mrecv_x, mrecv_yz)
     ix, iy, iz = lax.axis_index("gx"), lax.axis_index("gy"), lax.axis_index("gz")
-    me = (ix * ny + iy) * nz + iz
-
     load = pltpu.make_async_copy(u_hbm, own, own_sem)
     load.start()
 
-    def place(k):
-        target = lax.rem(me + k, devices)
-        return (lax.div(target, ny * nz), lax.rem(lax.div(target, nz), ny), lax.rem(target, nz))
-
     barrier = pltpu.get_barrier_semaphore()
 
     def wrap(value, size):
         return jnp.where(value >= size, value - size, value)
 
-    coordinates = [[wrap(index + k, size) for k in range(size)] if devices <= UNROLL else None
-                   for index, size in ((ix, nx), (iy, ny), (iz, nz))]
-
-    def everyone(act):
-        if devices > UNROLL:
-            def one(k, carry):
-                act(k - 1, place(k))
-                return carry
-            lax.fori_loop(1, devices, one, 0)
-            return
-        far = [(min(kx, nx - kx) + min(ky, ny - ky) + min(kz, nz - kz), kx, ky, kz)
-               for kx in range(nx) for ky in range(ny) for kz in range(nz)]
-        for _, kx, ky, kz in sorted(far, reverse=True)[:-1]:
-            act((kx * ny + ky) * nz + kz - 1, (coordinates[0][kx], coordinates[1][ky], coordinates[2][kz]))
-
-    everyone(lambda slot, device: pl.semaphore_signal(barrier, inc=1, device_id=device, device_id_type=MESH_ID))
+    coordinates = [[wrap(index + k, size) for k in range(size)] for index, size in ((ix, nx), (iy, ny), (iz, nz))]
+
+    def device_at(offset):
+        return tuple(coordinates[axis][offset[axis] % sizes[axis]] for axis in range(3))
+
+    def hops(offset):
+        return sum(min(k % size, -k % size) for k, size in zip(offset, sizes))
+
+    groups = [[(k, 0, 0) for k in range(1, nx)],
+              [(0, k // nz, k % nz) for k in range(1, ny * nz)]]
+    around = [(dx % nx, dy % ny, dz % nz) for dx in (-1, 0, 1) for dy in (-1, 0, 1) for dz in (-1, 0, 1)]
+    partners = sorted(set(around + groups[0] + groups[1]) - {(0, 0, 0)}, key=lambda o: (-hops(o), o))
+    for offset in partners:
+        pl.semaphore_signal(barrier, inc=1, device_id=device_at(offset), device_id_type=MESH_ID)
     load.wait()
 
     lane = lax.broadcasted_iota(jnp.int32, (ROWS, LANES), 1)
@@ -165,7 +156,7 @@
         speeds = signal_of([tiles[c][x] for c in range(COMPS)])
         best = speeds if best is None else jnp.maximum(best, speeds)
     best = jnp.max(jnp.where(lane < cz, best, 0.0), axis=0, keepdims=True)
-    msend[0] = best
+    msend[0, 0] = best
     packs = [[None, None] for _ in range(zsend.shape[1])]
     for c in range(COMPS):
         for x in range(cx):
@@ -184,13 +175,21 @@
         for pair in range(COMPS // 2):
             first, second = tiles[2 * pair][x], tiles[2 * pair + 1][x]
             swapped = pltpu.roll(second, GHOST, 0)
-            ysend[0, x, pair] = jnp.where(upper_half, first, swapped)
-            ysend[1, x, pair] = jnp.where(upper_half, swapped, first)
-        for c in range(COMPS):
-            y1send[0, x, c : c + 1] = tiles[c][x][0:1]
-            y1send[1, x, c : c + 1] = tiles[c][x][ROWS - 1 : ROWS]
-
-    pl.semaphore_wait(barrier, devices - 1)
+            below, above = jnp.where(upper_half, first, swapped), jnp.where(upper_half, swapped, first)
+            ysend[0, x, pair] = below
+            ysend[1, x, pair] = above
+            for side, plane in ((0, 0), (1, cx - 1)):
+                if x == plane:
+                    corner_send[0, side, pair] = below
+                    corner_send[1, side, pair] = above
+
+    for side, skipped in ((0, 0), (1, cx - 1)):
+        for number, x in enumerate(x for x in range(cx) if x != skipped):
+            for c in range(COMPS):
+                corner_send[0, side, COMPS // 2 + number, c : c + 1] = tiles[c][x][0:1]
+                corner_send[1, side, COMPS // 2 + number, c : c + 1] = tiles[c][x][ROWS - 1 : ROWS]
+
+    pl.semaphore_wait(barrier, len(partners))
 
     copies = []
     early, late = [], []
@@ -199,8 +198,7 @@
         number = len(copies)
         copy = pltpu.make_async_remote_copy(
             src_ref=src, dst_ref=dst, send_sem=send_sem.at[number], recv_sem=recv_sem.at[number],
-            device_id=(lax.rem(ix + dx + nx, nx), lax.rem(iy + dy + ny, ny), lax.rem(iz + dz + nz, nz)),
-            device_id_type=MESH_ID)
+            device_id=device_at((dx, dy, dz)), device_id_type=MESH_ID)
         copy.start()
         copies.append(copy)
         if dx:
@@ -208,33 +206,38 @@
         else:
             early.append(copy)
 
+    def share(turn, phase):
+        for slot, offset in enumerate(groups[phase]):
+            pltpu.make_async_remote_copy(
+                src_ref=msend.at[turn, phase], dst_ref=mrecv[phase].at[turn, slot],
+                send_sem=msend_sem.at[turn, phase], recv_sem=mrecv_sem.at[turn, phase],
+                device_id=device_at(offset), device_id_type=MESH_ID).start()
+
+    def gather(turn, phase):
+        held = mrecv[phase].at[turn]
+        pltpu.make_async_copy(held, held, mrecv_sem.at[turn, phase]).wait()
+        return jnp.maximum(jnp.max(held[...], axis=0), msend[turn, phase])
+
+    share(0, 0)
     for dx in (-1, 1):
         send(own, rx.at[(1 - dx) // 2], dx, 0, 0)
-
-    def share(turn):
-        everyone(lambda slot, device: pltpu.make_async_remote_copy(
-            src_ref=msend.at[turn], dst_ref=mrecv.at[turn, slot], send_sem=msend_sem.at[turn],
-            recv_sem=mrecv_sem.at[turn], device_id=device, device_id_type=MESH_ID).start())
-
-    def gather(turn):
-        pltpu.make_async_copy(mrecv.at[turn], mrecv.at[turn], mrecv_sem.at[turn]).wait()
-        pltpu.make_async_copy(mrecv.at[turn], mrecv.at[turn], msend_sem.at[turn]).wait()
-        return jnp.maximum(jnp.max(mrecv[turn], axis=0), msend[turn])
-
-    for dy in (-1, 1):
-        side = (dy + 1) // 2
-        for dx in (-1, 1):
-            corner = (1 - dx) // 2 * 2 + 1 - side
-            plane = 0 if dx == -1 else cx - 1
-            send(ysend.at[side, plane], rxy.at[corner], dx, dy, 0)
-            send(y1send.at[side], rxy1.at[corner], dx, dy, 0)
-        send(ysend.at[side], ry.at[1 - side], 0, dy, 0)
-    for dz in (-1, 1):
-        side = (dz + 1) // 2
-        for dx in (-1, 0, 1):
-            for dy in (-1, 0, 1):
+    for dy in (0, -1, 1):
+        for dz in (-1, 1):
+            side = (dz + 1) // 2
+            send(zsend.at[side], rz.at[1, 1 - dy, 1 - side], 0, dy, dz)
+        if dy:
+            side = (dy + 1) // 2
+            send(ysend.at[side], ry.at[1 - side], 0, dy, 0)
+    for dx in (-1, 1):
+        for dy in (-1, 1):
+            side = (dy + 1) // 2
+            send(corner_send.at[side, (dx + 1) // 2], rxy.at[(1 - dx) // 2 * 2 + 1 - side], dx, dy, 0)
+        for dy in (-1, 0, 1):
+            for dz in (-1, 1):
+                side = (dz + 1) // 2
                 send(zsend.at[side], rz.at[1 - dx, 1 - dy, 1 - side], dx, dy, dz)
-    share(0)
+    msend[0, 1] = gather(0, 0)
+    share(0, 1)
 
     for copy in early:
         copy.wait_recv()
@@ -267,7 +270,8 @@
                     side_tiles.append(jnp.where(upper_half, above, below))
                     side_tiles.append(pltpu.roll(jnp.where(upper_half, below, above), GHOST, 0))
             else:
-                below, above = rxy1[dx // 2 * 2, x], rxy1[dx // 2 * 2 + 1, x]
+                number = COMPS // 2 + (x if dx == 0 else x - 1)
+                below, above = rxy[dx // 2 * 2, number], rxy[dx // 2 * 2 + 1, number]
                 for c in range(COMPS):
                     side_tiles.append(jnp.where(upper_half, pltpu.roll(above, (-c) % ROWS, 0),
                                                 pltpu.roll(below, (ROWS - 1 - c) % ROWS, 0)))
@@ -313,7 +317,7 @@
             pred[axis, c, i] = flux[c] * half
 
     assemble(1)
-    now = gather(0)
+    now = gather(0, 1)
     dt = courant / jnp.max(now, axis=1, keepdims=True)
     step = jnp.broadcast_to(dt, (2 * ROWS, LANES))
     half = 0.5 * step
@@ -371,22 +375,28 @@
             out_ref[c, x] = total[x][c][:, 0:cz]
         speeds = signal_of(total[x])
         best = speeds if best is None else jnp.maximum(best, speeds)
-    msend[1] = jnp.max(jnp.where(in_body, best, 0.0), axis=0, keepdims=True)
-    share(1)
+    msend[1, 0] = jnp.max(jnp.where(in_body, best, 0.0), axis=0, keepdims=True)
+    share(1, 0)
     for copy in copies:
         copy.wait_send()
-    next_ref[0, 0] = courant / jnp.max(gather(1))
+    msend[1, 1] = gather(1, 0)
+    share(1, 1)
+    result = courant / jnp.max(gather(1, 1))
+    for turn in range(2):
+        for phase in range(2):
+            held = mrecv[phase].at[turn]
+            pltpu.make_async_copy(held, held, msend_sem.at[turn, phase]).wait()
+    next_ref[0, 0] = result
 
 
 def body(sizes, conserved_state):
     comps, cx, cy, cz = conserved_state.shape
     assert comps == COMPS and cx == GHOST and cy == ROWS and cz + 2 * GHOST <= LANES
-    devices = sizes[0] * sizes[1] * sizes[2]
     blocks = -(-COMPS * cx * GHOST // LANES)
     f32 = jnp.float32
     vmem = lambda *shape: pltpu.VMEM(shape, f32)
     pairs = COMPS // 2
-    messages = 2 + 8 + 2 + 18
+    messages = 2 + 4 + 2 + 18
     updated, following = pl.pallas_call(
         functools.partial(kernel, sizes),
         out_shape=(jax.ShapeDtypeStruct(conserved_state.shape, f32), jax.ShapeDtypeStruct((1, 1), f32)),
@@ -397,22 +407,22 @@
             vmem(2, COMPS, cx, cy, cz),
             vmem(2, cx, pairs, ROWS, LANES),
             vmem(2, cx, pairs, ROWS, LANES),
-            vmem(2, cx, ROWS, LANES),
+            vmem(2, 2, pairs + cx - 1, ROWS, LANES),
             vmem(2, blocks, ROWS, LANES),
             vmem(3, 3, 2, blocks, ROWS, LANES),
-            vmem(4, pairs, ROWS, LANES),
-            vmem(4, cx, ROWS, LANES),
+            vmem(4, pairs + cx - 1, ROWS, LANES),
             vmem(COMPS, cx, ROWS, LANES),
             vmem(COMPS, 3 * cx, 2 * ROWS, LANES),
             vmem(3, 2, COMPS, cx + 2, 2 * ROWS, LANES),
             vmem(3, COMPS, cx + 2, 2 * ROWS, LANES),
-            vmem(2, 1, LANES),
-            vmem(2, devices - 1, 1, LANES),
+            vmem(2, 2, 1, LANES),
+            vmem(2, sizes[0] - 1, 1, LANES),
+            vmem(2, sizes[1] * sizes[2] - 1, 1, LANES),
             pltpu.SemaphoreType.DMA,
             pltpu.SemaphoreType.DMA((messages,)),
             pltpu.SemaphoreType.DMA((messages,)),
-            pltpu.SemaphoreType.DMA((2,)),
-            pltpu.SemaphoreType.DMA((2,)),
+            pltpu.SemaphoreType.DMA((2, 2)),
+            pltpu.SemaphoreType.DMA((2, 2)),
         ],
         compiler_params=pltpu.CompilerParams(collective_id=0, has_side_effects=True),
     )(conserved_state)

time: 29.3 us -> 30.1 us (1.027)
  Pallas kernels: 25.2 us -> 25.9 us
    pallas_call x1, Pallas kernels: 25.2 us -> 25.9 us  [body(): pl.pallas_call(functools.partial(kernel, sizes), out_shape=(jax.ShapeDtyp...]
where the time goes in v3:
time: 30.1 us; the launch traced here: 29.9 us
  Pallas kernels  25.9 us (86%)
  between operations  2.46 us (8%)
  local copies, waits for them, and re-layouts  1.54 us (5%)
    pallas_call x1, Pallas kernels, body(): pl.pallas_call(functools.partial(kernel, sizes), out_shape=(jax.ShapeDtyp...  25.9 us
    unnamed x1, local copies, waits for them, and re-layouts  1.54 us

profile of v3, /device:TPU:0, one launch (start us, length us, event | category | flops | bytes accessed | tf_op | source)
XLA Modules:
  0.0 29.9 jit_solution(9558680936668446702)
XLA Ops:
  0.6 25.9 %shard_map.30 = (f32[6,4,8,120]{3,2,1,0:T(8,128)}, f32[1,1]{1,0:T(1,128)}) custom-call(f32[6,4,8,120]{3,2,1,0:T(8,128)} %u_hbm.1), custom_call_target="tpu_custom_call" | custom-call | tf_op jit(solution)/shard_map/pallas_call | solution.py:400
  26.6 1.5 %copy.5 = f32[6,4,8,120]{3,2,1,0:T(8,128)} copy(f32[6,4,8,120]{3,2,1,0:T(8,128)} %get-tuple-element.8) | data formatting | bytes 184320
